TPU v7x, 32 devices: a whole 2x2x4 slice. The times are simulated.
32 devices in a mesh: groups: 2 (over y), dp: 4 (over z), tensor: 4 (over x, core).
Axes of the slice: x: 2, y: 2, z: 4, core: 2. Of those that a mesh axis runs over, the one named last changes fastest.
Arguments:
- patches: bfloat16 [8192, 1280], P(('groups', 'dp')), parts along dimension 0, may hold values from -64 to 64
- grids: int32 [8, 2], P(('groups', 'dp')), parts along dimension 0, may hold values from 16 to 32, as said below
- dest: int32 [8, 256], P(('groups', 'dp')), parts along dimension 0, may hold values from 0 to 1535, as said below
- norm_gain: float32 [1280], replicated, may hold values from 0.1 to 1.9
- qkv_weight: bfloat16 [3, 1280, 1280], P(None, None, 'tensor'), may hold values from -8 to 8
- qkv_bias: float32 [3, 1280], P(None, 'tensor'), may hold values from -3 to 3
- proj_weight: bfloat16 [1280, 1280], P('tensor'), may hold values from -0.15625 to 0.15625
- proj_bias: float32 [1280], replicated, may hold values from -3 to 3
- merge_gain: float32 [1280], replicated, may hold values from 0.1 to 1.9
- w_first: bfloat16 [5120, 5120], P('dp', 'tensor'), may hold values from -0.078125 to 0.078125
- b_first: float32 [5120], P('tensor'), may hold values from -3 to 3
- w_second: bfloat16 [5120, 8192], P('tensor', 'dp'), may hold values from -0.078125 to 0.078125
- b_second: float32 [8192], P('tensor'), may hold values from -3 to 3
- text_embed: bfloat16 [3072, 8192], P(('groups', 'dp'), 'tensor'), parts along dimension 0, may hold values from -6 to 6
Outputs:
- sequence: bfloat16 [3072, 8192], P(('groups', 'dp'), 'tensor'), parts along dimension 0
There are 2 independent parts, one for each index of `groups`. A program takes and returns all parts, laid end to end along the dimension named above; an argument that names none is the same for every part. Nothing has to cross between parts.
Inputs may be any that keep to these rules, and one draw needn't show every extreme that they name: `grids`: both sides of every grid are even, at least 16 and at most 32; in each part along `groups`, the first image (the one on dp index 0) has the full 32 x 32 grid. The rows dest[i, j] with j < grids[i, 0] * grids[i, 1] / 4 are distinct over all images; the live rows of one image reach at most 64 rows in each aligned block of 384 sequence rows, and exactly that many for a full grid.
All inputs are finite; a program needn't handle non-finite values.
Results may differ from a plain program's by a relative error of at most 0.014.
Values may be sent and summed in bfloat16 or wider, within the bound.
A program may use at most 128 MiB of HBM per device.

v0:
```python
import math
import jax
import jax.numpy as jnp
from jax import lax
from jax.sharding import PartitionSpec as P

HEAD_DIM = 80
PATCHES = 1024
MERGED = 256


def rms_scale(values, gain):
    return values * lax.rsqrt(jnp.mean(values * values, axis=-1, keepdims=True) + 1e-06) * gain


def local(
    patches,
    grids,
    dest,
    norm_gain,
    qkv_weight,
    qkv_bias,
    proj_weight,
    proj_bias,
    merge_gain,
    w_first,
    b_first,
    w_second,
    b_second,
    text_embed,
):
    rows_dev = patches.shape[0]
    images_dev = grids.shape[0]
    heads_dev = qkv_weight.shape[2] // HEAD_DIM
    live_count = grids[:, 0] * grids[:, 1]
    normed = rms_scale(patches.astype(jnp.float32), norm_gain).astype(jnp.bfloat16)
    projected = (
        jnp.einsum("rv,jvc->jrc", normed, qkv_weight, preferred_element_type=jnp.float32)
        + qkv_bias[:, None, :]
    )
    projected = projected.astype(jnp.bfloat16).reshape(3, images_dev, PATCHES, heads_dev, HEAD_DIM)
    scores = jnp.einsum(
        "iqhd,ikhd->ihqk", projected[0], projected[1], preferred_element_type=jnp.float32
    ) / math.sqrt(HEAD_DIM)
    live_keys = jnp.arange(PATCHES, dtype=jnp.int32)[None, :] < live_count[:, None]
    scores = jnp.where(live_keys[:, None, None, :], scores, jnp.float32(-1e30))
    peak_score = jnp.max(scores, axis=-1, keepdims=True)
    exponent = jnp.exp(scores - peak_score)
    weights = (exponent / jnp.sum(exponent, axis=-1, keepdims=True)).astype(jnp.bfloat16)
    attended = jnp.einsum(
        "ihqk,ikhd->iqhd", weights, projected[2], preferred_element_type=jnp.float32
    )
    attended = attended.astype(jnp.bfloat16).reshape(rows_dev, heads_dev * HEAD_DIM)
    partial_value = jnp.dot(attended, proj_weight, preferred_element_type=jnp.float32).astype(
        jnp.bfloat16
    )
    summed = lax.psum(partial_value, "tensor").astype(jnp.float32)
    resid = patches.astype(jnp.float32) + summed + proj_bias
    merged_in = rms_scale(resid, merge_gain).astype(jnp.bfloat16)
    merged_in = merged_in.reshape(rows_dev // 4, 4 * patches.shape[1])
    merged_dev = merged_in.shape[0]
    received = lax.all_to_all(merged_in, "dp", split_axis=1, concat_axis=0, tiled=True)
    first_out = lax.psum_scatter(
        jnp.dot(received, w_first, preferred_element_type=jnp.float32).astype(jnp.bfloat16),
        "dp",
        scatter_dimension=0,
        tiled=True,
    ).astype(jnp.float32)
    hidden = jax.nn.gelu(first_out + b_first, approximate=False).astype(jnp.bfloat16)
    second_rows = jnp.dot(
        hidden,
        lax.all_gather(w_second, "dp", axis=1, tiled=True),
        preferred_element_type=jnp.float32,
    ).astype(jnp.bfloat16)
    visual = lax.psum_scatter(second_rows, "tensor", scatter_dimension=1, tiled=True).astype(
        jnp.float32
    )
    visual = (visual + b_second).astype(jnp.bfloat16)
    feature_count = visual.shape[1]
    dp_count = lax.axis_size("dp")
    seq_rows = text_embed.shape[0]
    capacity = images_dev * (MERGED // dp_count)
    live_rows = (jnp.arange(MERGED, dtype=jnp.int32)[None, :] < (live_count // 4)[:, None]).reshape(
        merged_dev
    )
    dest_flat = dest.reshape(merged_dev)
    shard_id = jnp.where(live_rows, dest_flat // seq_rows, dp_count)
    local_row = dest_flat % seq_rows
    one_hot = (shard_id[:, None] == jnp.arange(dp_count, dtype=jnp.int32)[None, :]).astype(
        jnp.int32
    )
    before = jnp.cumsum(one_hot, axis=0) - one_hot
    slot_index = jnp.sum(before * one_hot, axis=1)
    buffer = (
        jnp.zeros((dp_count, capacity, feature_count), jnp.bfloat16)
        .at[shard_id, slot_index]
        .set(visual, mode="drop")
    )
    positions = (
        jnp.full((dp_count, capacity), seq_rows, jnp.int32)
        .at[shard_id, slot_index]
        .set(local_row, mode="drop")
    )
    arrived, arrived_rows = (
        lax.all_to_all(buffer, "dp", split_axis=0, concat_axis=0, tiled=True),
        lax.all_to_all(positions, "dp", split_axis=0, concat_axis=0, tiled=True),
    )
    sequence = text_embed.at[arrived_rows.reshape(-1)].set(
        arrived.reshape(-1, feature_count), mode="drop"
    )
    return sequence


def solution(mesh):
    in_specs = (
        P(("groups", "dp"), None),
        P(("groups", "dp"), None),
        P(("groups", "dp"), None),
        P(),
        P(None, None, "tensor"),
        P(None, "tensor"),
        P("tensor", None),
        P(),
        P(),
        P("dp", "tensor"),
        P("tensor"),
        P("tensor", "dp"),
        P("tensor"),
        P(("groups", "dp"), "tensor"),
    )
    out_specs = P(("groups", "dp"), "tensor")
    return jax.shard_map(local, mesh=mesh, in_specs=in_specs, out_specs=out_specs, check_vma=False)
```

profile of v0, /device:TPU:0, one launch (start us, length us, event | category | flops | bytes accessed | tf_op | source)
XLA Modules:
  0.0 749.1 jit_solution(11529100986900097305)
XLA Ops:
  6.5 2.9 copy.35
  9.4 0.7 fusion.104
  11.4 0.0 copy-start.10
  11.4 0.0 copy-start.12
  11.4 0.6 fusion.6
  12.0 1.1 copy-done.10
  13.1 2.9 fusion.15
  15.9 1.3 fusion.103
  17.3 10.9 %fusion.105 = (f32[4,1024]{1,0:T(4,128)S(1)}, f32[4,1024,1024]{1,2,0:T(8,128)}) fusion(pred[1024]{0:T(1024)(128)(4,1)S(1)} %iota_compare_fusion, bf16[1024,4,80]{0,2,1:T(8,128)(2,1)} %bitcast.76, bf16[1024,4,80]{0,2,1:T(8,128)(2,1)} %bitcast.75), kind=kOutput, calls=%fused_computation.150 | convolution fusion | flops 687866880 | bytes 18105344 | tf_op jit(solution)/shard_map/sub | solution.py:48
  28.1 7.6 %fusion.20 = bf16[4,80,1024]{2,1,0:T(8,128)(2,1)S(1)} fusion(bf16[1024,4,80]{0,2,1:T(8,128)(2,1)} %bitcast.74, f32[4,1024,1024]{1,2,0:T(8,128)} %get-tuple-element.17, f32[4,1024]{1,0:T(4,128)S(1)} %get-tuple-element.16), kind=kOutput, calls=%fused_computation.33 | convolution fusion | flops 679804928 | bytes 18104320 | tf_op jit(solution)/shard_map/ihqk,ikhd->iqhd/dot_general | solution.py:50
  35.8 3.1 convolution_convert_fusion.2
  38.9 0.0 all-reduce.2.cloned.1.call-update
  38.9 0.2 reduce-scatter.3.cloned.1.call-start
  39.1 62.5 %all-reduce.2.cloned.1.call-done = bf16[1024,1280]{1,0:T(8,128)(2,1)} async-done(((bf16[1024,1280]{1,0:T(8,128)(2,1)}), bf16[1024,1280]{1,0:T(8,128)(2,1)}) %all-reduce.2.cloned.1.call-update) | async-done | bytes 2621456 | tf_op jit(solution)/shard_map/psum | solution.py:57
  101.7 3.8 multiply_reduce_fusion
  105.5 0.3 copy-done.4
  105.8 2.6 multiply_convert_fusion
  108.4 5.6 all_to_all.25
  114.0 2.1 copy.26
  116.0 63.6 %all_to_all.33 = bf16[256,4,1280]{2,0,1:T(8,128)(2,1)S(1)} all-to-all(bf16[256,4,1280]{2,0,1:T(8,128)(2,1)S(1)} %copy.26), channel_id=1, replica_groups=mesh['groups'=2,'dp'=4,'tensor'=4] {'dp'}, dimensions={1} | all-to-all | bytes 5242880 | tf_op jit(solution)/shard_map/all_to_all | solution.py:62
  179.6 4.9 convolution_convert_fusion.1
  184.5 0.0 reduce-scatter.3.cloned.1.call-update
  184.5 0.0 all-gather.2.cloned.1.call-start
  184.5 0.7 all-gather.2.cloned.1.call-update
  185.2 0.0 reduce-scatter.5.cloned.1.call-start
  185.3 50.0 %reduce-scatter.3.cloned.1.call-done = bf16[256,1280]{1,0:T(8,128)(2,1)} async-done(((bf16[1024,1280]{1,0:T(8,128)(2,1)}), bf16[256,1280]{1,0:T(8,128)(2,1)}) %reduce-scatter.3.cloned.1.call-update) | async-done | bytes 655376 | tf_op jit(solution)/shard_map/reduce_scatter | solution.py:63
  235.3 358.0 %all-gather.2.cloned.1.call-done = bf16[1280,8192]{1,0:T(8,128)(2,1)} async-done(((bf16[1280,2048]{1,0:T(8,128)(2,1)}), bf16[1280,8192]{1,0:T(8,128)(2,1)}) %all-gather.2.cloned.1.call-update) | async-done | bytes 20971536 | tf_op jit(solution)/shard_map/all_gather | solution.py:72
  593.3 17.4 %convolution_convert_fusion = bf16[256,8192]{1,0:T(8,128)(2,1)} fusion(bf16[1280,8192]{1,0:T(8,128)(2,1)} %all-gather.2.cloned.1.call-done, bf16[256,1280]{1,0:T(8,128)(2,1)} %reduce-scatter.3.cloned.1.call-done, f32[1280]{0:T(1024)S(1)} %copy-done.13), kind=kOutput, calls=%fused_computation.8 | convolution fusion | flops 5392760832 | bytes 25826304 | tf_op jit(solution)/shard_map/dot_general | solution.py:70
  610.7 0.0 reduce-scatter.5.cloned.1.call-update
  610.7 0.6 copy-done.6
  611.4 1.2 reduce-window.6
  612.7 0.1 slice.35
  612.7 0.1 copy.22
  612.9 0.1 copy.23
  613.0 0.1 add_bitcast_fusion
  613.1 0.6 broadcast_in_dim.23
  613.7 38.8 %scatter_fusion = s32[4,64]{1,0:T(4,128)} fusion(s32[4,64]{1,0:T(4,128)} %broadcast_in_dim.23, s32[256]{0:T(256)S(1)} %bitcast.71, s32[256]{0:T(256)S(1)} %get-tuple-element.10), kind=kCustom, calls=%fused_computation | custom fusion | bytes 5120 | tf_op jit(solution)/shard_map/scatter | solution.py:102
  652.5 3.2 all-to-all-start
  655.7 0.0 reduce-scatter.5.cloned.1.call-done
  655.7 1.5 add_convert_fusion.1
  657.2 1.2 broadcast_in_dim.28
  658.4 48.1 %scatter_fusion.1 = bf16[4,64,2048]{2,1,0:T(8,128)(2,1)} fusion(bf16[4,64,2048]{2,1,0:T(8,128)(2,1)} %broadcast_in_dim.28, s32[256]{0:T(256)S(1)} %bitcast.72, bf16[256,2048]{1,0:T(8,128)(2,1)S(1)} %add_convert_fusion.1), kind=kCustom, calls=%fused_computation.1 | custom fusion | bytes 3147776 | tf_op jit(solution)/shard_map/scatter | solution.py:97
  706.5 5.0 all-to-all-start.2
  711.5 0.5 broadcast.284
  712.0 0.6 reduce.11
  712.7 0.1 reshape.264
  712.8 24.2 %all-to-all-done.2 = bf16[4,64,2048]{2,1,0:T(8,128)(2,1)} async-done(((bf16[4,64,2048]{2,1,0:T(8,128)(2,1)}), bf16[4,64,2048]{2,1,0:T(8,128)(2,1)}, u32[]{:S(2)}, u32[]{:S(2)}) %all-to-all-start.2) | async-done | bytes 1048608 | tf_op jit(solution)/shard_map/all_to_all | solution.py:105
  736.9 5.7 scatter_fusion.2
  (40 shorter events, 0.2 us)
Async XLA Ops:
  6.5 173.1 %copy-start = (bf16[1280,1280]{1,0:T(8,128)(2,1)S(1)}, bf16[1280,1280]{1,0:T(8,128)(2,1)}, u32[]{:S(2)}) copy-start(bf16[1280,1280]{1,0:T(8,128)(2,1)} %param.23) | copy-start | bytes 9830404
  6.5 2.9 copy-start.9
  6.5 95.1 %all-reduce.2.cloned.1.call-start = ((), (), s32[]{:S(2)}) async-start(), calls=%async_computation.5 | async-start | bytes 5242880 | tf_op jit(solution)/shard_map/psum | solution.py:57
  6.5 4.8 copy-start.2
  11.4 1.7 copy-start.10
  11.4 1.7 copy-start.12
  11.4 1.7 copy-start.14
  28.1 7.6 %copy-start.11 = (bf16[320,1280]{1,0:T(8,128)(2,1)S(1)}, bf16[320,1280]{1,0:T(8,128)(2,1)}, u32[]{:S(2)}) copy-start(bf16[320,1280]{1,0:T(8,128)(2,1)} %param.20) | copy-start | bytes 2457604
  38.9 62.8 %copy-start.5 = (f32[1280]{0:T(1024)S(1)}, f32[1280]{0:T(1024)}, u32[]{:S(2)}) copy-start(f32[1280]{0:T(1024)} %param.21) | copy-start | bytes 15364
  38.9 66.6 %copy-start.7 = (f32[1280]{0:T(1024)S(1)}, f32[1280]{0:T(1024)}, u32[]{:S(2)}) copy-start(f32[1280]{0:T(1024)} %param.22) | copy-start | bytes 15364
  38.9 196.4 %reduce-scatter.3.cloned.1.call-start = ((), (), s32[]{:S(2)}) async-start(), calls=%async_computation.6 | async-start | bytes 3276800 | tf_op jit(solution)/shard_map/reduce_scatter | solution.py:63
  101.7 3.8 copy-start.3
  101.7 4.1 copy-start.4
  184.5 408.8 %copy-start.13 = (f32[1280]{0:T(1024)S(1)}, f32[1280]{0:T(1024)}, u32[]{:S(2)}) copy-start(f32[1280]{0:T(1024)} %param.24) | copy-start | bytes 15364
  184.5 408.8 %all-gather.2.cloned.1.call-start = ((), (), s32[]{:S(2)}) async-start(), calls=%async_computation.7 | async-start | bytes 26214400 | tf_op jit(solution)/shard_map/all_gather | solution.py:72
  185.2 470.5 %reduce-scatter.5.cloned.1.call-start = ((), (), s32[]{:S(2)}) async-start(), calls=%async_computation.8 | async-start | bytes 5242880 | tf_op jit(solution)/shard_map/reduce_scatter | solution.py:75
  610.7 0.7 copy-start.6
  610.7 45.0 %copy-start.8 = (f32[2048]{0:T(1024)S(1)}, f32[2048]{0:T(1024)}, u32[]{:S(2)}) copy-start(f32[2048]{0:T(1024)} %param.26) | copy-start | bytes 24580
  652.5 54.0 %all-to-all-start = ((s32[4,1,64]{2,1,0:T(1,128)}), s32[4,1,64]{2,1,0:T(1,128)S(1)}, u32[]{:S(2)}, u32[]{:S(2)}) async-start(s32[4,1,64]{2,1,0:T(1,128)} %bitcast.12), calls=%async_computation | async-start | bytes 4096 | tf_op jit(solution)/shard_map/all_to_all | solution.py:106
  706.5 30.4 %all-to-all-start.2 = ((bf16[4,64,2048]{2,1,0:T(8,128)(2,1)}), bf16[4,64,2048]{2,1,0:T(8,128)(2,1)}, u32[]{:S(2)}, u32[]{:S(2)}) async-start(bf16[4,64,2048]{2,1,0:T(8,128)(2,1)} %scatter_fusion.1), calls=%async_computation.4 | async-start | bytes 2097152 | tf_op jit(solution)/shard_map/all_to_all | solution.py:105
  736.9 5.7 copy-start.1
Sparse Core Ops, SparseCore 0:
  39.0 62.6 all-reduce.1
  184.6 50.6 reduce-scatter.2
  236.9 356.3 all-gather.1
  610.8 42.9 reduce-scatter.4
where the time goes:
time: 753 us; the launch traced here: 749 us
  waiting for transfers between devices  495 us (66%)
  local copies, waits for them, and re-layouts  110 us (15%)
  blocking collectives  63.6 us (8%)
  matrix products  46.7 us (6%)
  between operations  14.6 us (2%)
  other arithmetic  10.6 us (1%)
  starting transfers between devices  8.51 us (1%)
    all_gather x1, waiting for transfers between devices, local(): lax.all_gather(w_second, 'dp', axis=1, tiled=True)  358 us
    all_to_all x1, blocking collectives, local(): lax.all_to_all(merged_in, 'dp', split_axis=1, concat_axis=0, tiled=True)  63.6 us
    psum x1, waiting for transfers between devices, local(): summed = lax.psum(partial_value, 'tensor').astype(jnp.float32)  62.5 us
    reduce_scatter x1, waiting for transfers between devices, local(): lax.psum_scatter(jnp.dot(received, w_first, preferred_element_type=jnp.fl...  50 us
    scatter x1, local copies, waits for them, and re-layouts, local(): buffer = jnp.zeros((dp_count, capacity, feature_count), jnp.bfloat16).at[...  48.1 us
    scatter x1, local copies, waits for them, and re-layouts, local(): positions = jnp.full((dp_count, capacity), seq_rows, jnp.int32).at[shard_...  38.8 us
    all_to_all x1, waiting for transfers between devices, local(): lax.all_to_all(buffer, 'dp', split_axis=0, concat_axis=0, tiled=True)  24.2 us
    dot_general x1, matrix products, local(): jnp.dot(hidden, lax.all_gather(w_second, 'dp', axis=1, tiled=True), prefe...  17.4 us
  transfers between devices with their start and end apart: 6, of which 4 were waited for; matrix products, arithmetic and copies ran while one was open for 12% of the time, Pallas kernels for 0%

commit v1 on v0

--- a/solution.py
+++ b/solution.py
@@ -3,6 +3,7 @@
 import jax.numpy as jnp
 from jax import lax
 from jax.sharding import PartitionSpec as P
+from jax.lax import all_gather
 
 HEAD_DIM = 80
 PATCHES = 1024
@@ -68,9 +69,7 @@
     ).astype(jnp.float32)
     hidden = jax.nn.gelu(first_out + b_first, approximate=False).astype(jnp.bfloat16)
     second_rows = jnp.dot(
-        hidden,
-        lax.all_gather(w_second, "dp", axis=1, tiled=True),
-        preferred_element_type=jnp.float32,
+        hidden, jnp.concatenate(all_gather(w_second, "dp"), 1), preferred_element_type=jnp.float32
     ).astype(jnp.bfloat16)
     visual = lax.psum_scatter(second_rows, "tensor", scatter_dimension=1, tiled=True).astype(
         jnp.float32

time: 753 us -> 668 us (0.89)
  waiting for transfers between devices: 495 us -> 304 us
  blocking collectives: 63.6 us -> 143 us
  local copies, waits for them, and re-layouts: 110 us -> 136 us
    all_gather x1, waiting for transfers between devices: 358 us -> 192 us  [local(): all_gather(w_second, 'dp')]
    all_to_all x1, blocking collectives: 63.6 us -> 143 us  [local(): lax.all_to_all(merged_in, 'dp', split_axis=1, concat_axis=0, tiled=True)]
    reshape x0 -> x1, local copies, waits for them, and re-layouts: none -> 27.7 us  [local(): jnp.concatenate(all_gather(w_second, 'dp'), 1)]
    reduce_scatter x1, waiting for transfers between devices: 50 us -> 25.2 us  [local(): lax.psum_scatter(jnp.dot(received, w_first, preferred_element_type=jnp.fl...]
  transfers between devices with their start and end apart: 6 -> 6, of which waited for: 4 -> 4; matrix products, arithmetic and copies ran while one was open for 12% -> 20% of each run, Pallas kernels for 0% -> 0%
where the time goes in v1:
time: 668 us; the launch traced here: 664 us
  waiting for transfers between devices  304 us (46%)
  blocking collectives  143 us (21%)
  local copies, waits for them, and re-layouts  136 us (20%)
  matrix products  45.7 us (7%)
  between operations  16.4 us (2%)
  other arithmetic  10.6 us (2%)
  starting transfers between devices  8.54 us (1%)
    all_gather x1, waiting for transfers between devices, local(): all_gather(w_second, 'dp')  192 us
    all_to_all x1, blocking collectives, local(): lax.all_to_all(merged_in, 'dp', split_axis=1, concat_axis=0, tiled=True)  143 us
    psum x1, waiting for transfers between devices, local(): summed = lax.psum(partial_value, 'tensor').astype(jnp.float32)  62 us
    scatter x1, local copies, waits for them, and re-layouts, local(): buffer = jnp.zeros((dp_count, capacity, feature_count), jnp.bfloat16).at[...  48.1 us
    scatter x1, local copies, waits for them, and re-layouts, local(): positions = jnp.full((dp_count, capacity), seq_rows, jnp.int32).at[shard_...  38.2 us
    reshape x1, local copies, waits for them, and re-layouts, local(): jnp.concatenate(all_gather(w_second, 'dp'), 1)  27.7 us
    reduce_scatter x1, waiting for transfers between devices, local(): lax.psum_scatter(jnp.dot(received, w_first, preferred_element_type=jnp.fl...  25.2 us
    all_to_all x1, waiting for transfers between devices, local(): lax.all_to_all(buffer, 'dp', split_axis=0, concat_axis=0, tiled=True)  23.8 us
  transfers between devices with their start and end apart: 6, of which 4 were waited for; matrix products, arithmetic and copies ran while one was open for 20% of the time, Pallas kernels for 0%

profile of v1, /device:TPU:0, one launch (start us, length us, event | category | flops | bytes accessed | tf_op | source)
XLA Modules:
  0.0 664.0 jit_solution(1881379058950404054)
XLA Ops:
  7.4 2.9 copy.41
  10.3 0.7 fusion.104
  12.3 0.6 fusion.6
  12.9 2.9 fusion.15
  15.8 1.3 fusion.103
  17.1 10.9 %fusion.105 = (f32[4,1024]{1,0:T(4,128)S(1)}, f32[4,1024,1024]{1,2,0:T(8,128)}) fusion(pred[1024]{0:T(1024)(128)(4,1)S(1)} %iota_compare_fusion, bf16[1024,4,80]{0,2,1:T(8,128)(2,1)} %bitcast.85, bf16[1024,4,80]{0,2,1:T(8,128)(2,1)} %bitcast.84), kind=kOutput, calls=%fused_computation.150 | convolution fusion | flops 687866880 | bytes 18105344 | tf_op jit(solution)/shard_map/sub | solution.py:49
  28.0 7.6 %fusion.20 = bf16[4,80,1024]{2,1,0:T(8,128)(2,1)S(1)} fusion(bf16[1024,4,80]{0,2,1:T(8,128)(2,1)} %bitcast.83, f32[4,1024,1024]{1,2,0:T(8,128)} %get-tuple-element.17, f32[4,1024]{1,0:T(4,128)S(1)} %get-tuple-element.16), kind=kOutput, calls=%fused_computation.33 | convolution fusion | flops 679804928 | bytes 18104320 | tf_op jit(solution)/shard_map/ihqk,ikhd->iqhd/dot_general | solution.py:51
  35.7 3.1 convolution_convert_fusion.2
  38.8 0.0 all-reduce.2.cloned.1.call-update
  38.8 0.0 copy-start.5
  38.8 0.0 all-gather.3.cloned.1.call-start
  38.8 0.5 all-gather.3.cloned.1.call-update
  39.4 0.0 copy-start.7
  39.4 0.2 reduce-scatter.3.cloned.1.call-start
  39.6 62.0 %all-reduce.2.cloned.1.call-done = bf16[1024,1280]{1,0:T(8,128)(2,1)} async-done(((bf16[1024,1280]{1,0:T(8,128)(2,1)}), bf16[1024,1280]{1,0:T(8,128)(2,1)}) %all-reduce.2.cloned.1.call-update) | async-done | bytes 2621456 | tf_op jit(solution)/shard_map/psum | solution.py:58
  101.6 3.8 multiply_reduce_fusion
  105.4 0.3 copy-done.4
  105.7 2.7 multiply_convert_fusion
  108.3 5.6 all_to_all.25
  113.9 2.1 copy.31
  116.0 143.4 %all_to_all.33 = bf16[256,4,1280]{2,0,1:T(8,128)(2,1)S(1)} all-to-all(bf16[256,4,1280]{2,0,1:T(8,128)(2,1)S(1)} %copy.31), channel_id=1, replica_groups=mesh['groups'=2,'dp'=4,'tensor'=4] {'dp'}, dimensions={1} | all-to-all | bytes 5242880 | tf_op jit(solution)/shard_map/all_to_all | solution.py:63
  259.4 4.8 convolution_convert_fusion.1
  264.3 0.0 reduce-scatter.3.cloned.1.call-update
  264.3 0.0 reduce-scatter.5.cloned.1.call-start
  264.4 191.9 %all-gather.3.cloned.1.call-done = bf16[5120,2048]{1,0:T(8,128)(2,1)} async-done(((bf16[1280,2048]{1,0:T(8,128)(2,1)}), bf16[5120,2048]{1,0:T(8,128)(2,1)}) %all-gather.3.cloned.1.call-update) | async-done | bytes 20971536 | tf_op jit(solution)/shard_map/all_gather | solution.py:72
  456.3 27.7 %copy.32 = bf16[1280,4,2048]{0,2,1:T(8,128)(2,1)} copy(bf16[1280,4,2048]{2,0,1:T(8,128)(2,1)} %bitcast.80) | data formatting | bytes 41943040 | tf_op jit(solution)/shard_map/reshape | solution.py:72
  483.9 25.2 %reduce-scatter.3.cloned.1.call-done = bf16[256,1280]{1,0:T(8,128)(2,1)} async-done(((bf16[1024,1280]{1,0:T(8,128)(2,1)}), bf16[256,1280]{1,0:T(8,128)(2,1)}) %reduce-scatter.3.cloned.1.call-update) | async-done | bytes 655376 | tf_op jit(solution)/shard_map/reduce_scatter | solution.py:64
  509.2 16.4 %convolution_convert_fusion = bf16[256,8192]{1,0:T(8,128)(2,1)} fusion(bf16[1280,8192]{0,1:T(8,128)(2,1)} %bitcast.81, bf16[256,1280]{1,0:T(8,128)(2,1)} %reduce-scatter.3.cloned.1.call-done, f32[1280]{0:T(1024)S(1)} %copy-done.13), kind=kOutput, calls=%fused_computation.8 | convolution fusion | flops 5392760832 | bytes 25826304 | tf_op jit(solution)/shard_map/dot_general | solution.py:71
  525.6 0.0 reduce-scatter.5.cloned.1.call-update
  525.7 0.6 copy-done.6
  526.4 1.2 reduce-window.6
  527.6 0.1 slice.35
  527.7 0.1 copy.27
  527.8 0.1 copy.28
  527.9 0.1 add_bitcast_fusion
  528.0 0.6 broadcast_in_dim.23
  528.6 38.2 %scatter_fusion = s32[4,64]{1,0:T(4,128)} fusion(s32[4,64]{1,0:T(4,128)} %broadcast_in_dim.23, s32[256]{0:T(256)S(1)} %bitcast.78, s32[256]{0:T(256)S(1)} %get-tuple-element.10), kind=kCustom, calls=%fused_computation | custom fusion | bytes 5120 | tf_op jit(solution)/shard_map/scatter | solution.py:101
  566.8 3.4 all-to-all-start
  570.2 0.0 reduce-scatter.5.cloned.1.call-done
  570.3 1.5 add_convert_fusion.1
  571.8 1.2 broadcast_in_dim.28
  572.9 48.1 %scatter_fusion.1 = bf16[4,64,2048]{2,1,0:T(8,128)(2,1)} fusion(bf16[4,64,2048]{2,1,0:T(8,128)(2,1)} %broadcast_in_dim.28, s32[256]{0:T(256)S(1)} %bitcast.79, bf16[256,2048]{1,0:T(8,128)(2,1)S(1)} %add_convert_fusion.1), kind=kCustom, calls=%fused_computation.1 | custom fusion | bytes 3147776 | tf_op jit(solution)/shard_map/scatter | solution.py:96
  621.0 4.8 all-to-all-start.2
  625.8 0.5 broadcast.284
  626.4 0.6 reduce.11
  627.0 0.1 reshape.270
  627.1 23.8 %all-to-all-done.2 = bf16[4,64,2048]{2,1,0:T(8,128)(2,1)} async-done(((bf16[4,64,2048]{2,1,0:T(8,128)(2,1)}), bf16[4,64,2048]{2,1,0:T(8,128)(2,1)}, u32[]{:S(2)}, u32[]{:S(2)}) %all-to-all-start.2) | async-done | bytes 1048608 | tf_op jit(solution)/shard_map/all_to_all | solution.py:104
  650.9 5.7 scatter_fusion.2
  (41 shorter events, 0.2 us)
Async XLA Ops:
  7.4 252.1 %copy-start = (bf16[1280,1280]{1,0:T(8,128)(2,1)S(1)}, bf16[1280,1280]{1,0:T(8,128)(2,1)}, u32[]{:S(2)}) copy-start(bf16[1280,1280]{1,0:T(8,128)(2,1)} %param.23) | copy-start | bytes 9830404
  7.4 2.9 copy-start.9
  7.4 94.2 %all-reduce.2.cloned.1.call-start = ((), (), s32[]{:S(2)}) async-start(), calls=%async_computation.5 | async-start | bytes 5242880 | tf_op jit(solution)/shard_map/psum | solution.py:58
  7.4 4.9 copy-start.2
  10.3 2.6 copy-start.10
  10.3 2.7 copy-start.12
  10.3 2.7 copy-start.14
  28.0 7.6 %copy-start.11 = (bf16[320,1280]{1,0:T(8,128)(2,1)S(1)}, bf16[320,1280]{1,0:T(8,128)(2,1)}, u32[]{:S(2)}) copy-start(bf16[320,1280]{1,0:T(8,128)(2,1)} %param.20) | copy-start | bytes 2457604
  38.8 62.8 %copy-start.5 = (f32[1280]{0:T(1024)S(1)}, f32[1280]{0:T(1024)}, u32[]{:S(2)}) copy-start(f32[1280]{0:T(1024)} %param.21) | copy-start | bytes 15364
  38.8 417.5 %all-gather.3.cloned.1.call-start = ((), (), s32[]{:S(2)}) async-start(), calls=%async_computation.8 | async-start | bytes 26214400 | tf_op jit(solution)/shard_map/all_gather | solution.py:72
  39.4 66.0 %copy-start.7 = (f32[1280]{0:T(1024)S(1)}, f32[1280]{0:T(1024)}, u32[]{:S(2)}) copy-start(f32[1280]{0:T(1024)} %param.22) | copy-start | bytes 15364
  39.4 469.8 %reduce-scatter.3.cloned.1.call-start = ((), (), s32[]{:S(2)}) async-start(), calls=%async_computation.6 | async-start | bytes 3276800 | tf_op jit(solution)/shard_map/reduce_scatter | solution.py:64
  101.6 3.8 copy-start.3
  101.6 4.1 copy-start.4
  264.3 305.9 %reduce-scatter.5.cloned.1.call-start = ((), (), s32[]{:S(2)}) async-start(), calls=%async_computation.7 | async-start | bytes 5242880 | tf_op jit(solution)/shard_map/reduce_scatter | solution.py:74
  456.3 52.9 %copy-start.13 = (f32[1280]{0:T(1024)S(1)}, f32[1280]{0:T(1024)}, u32[]{:S(2)}) copy-start(f32[1280]{0:T(1024)} %param.24) | copy-start | bytes 15364
  525.6 0.7 copy-start.6
  525.6 44.6 %copy-start.8 = (f32[2048]{0:T(1024)S(1)}, f32[2048]{0:T(1024)}, u32[]{:S(2)}) copy-start(f32[2048]{0:T(1024)} %param.26) | copy-start | bytes 24580
  566.8 54.2 %all-to-all-start = ((s32[4,1,64]{2,1,0:T(1,128)}), s32[4,1,64]{2,1,0:T(1,128)S(1)}, u32[]{:S(2)}, u32[]{:S(2)}) async-start(s32[4,1,64]{2,1,0:T(1,128)} %bitcast.12), calls=%async_computation | async-start | bytes 4096 | tf_op jit(solution)/shard_map/all_to_all | solution.py:105
  621.0 29.9 %all-to-all-start.2 = ((bf16[4,64,2048]{2,1,0:T(8,128)(2,1)}), bf16[4,64,2048]{2,1,0:T(8,128)(2,1)}, u32[]{:S(2)}, u32[]{:S(2)}) async-start(bf16[4,64,2048]{2,1,0:T(8,128)(2,1)} %scatter_fusion.1), calls=%async_computation.4 | async-start | bytes 2097152 | tf_op jit(solution)/shard_map/all_to_all | solution.py:104
  650.9 5.7 copy-start.1
Sparse Core Ops, SparseCore 0:
  38.9 62.6 all-reduce.1
  525.8 43.9 reduce-scatter.4
Sparse Core Ops, SparseCore 1:
  40.9 415.4 all-gather.2
  458.5 50.7 reduce-scatter.2
